TPU v7x, 32 devices: a whole 2x2x4 slice. The times are simulated.
32 devices in a mesh: param: 4 (over y, x), dom: 8 (over z, core).
Axes of the slice: x: 2, y: 2, z: 4, core: 2. Of those that a mesh axis runs over, the one named last changes fastest.
Arguments:
- particles: bfloat16 [128, 524288], P('dom', 'param'), may hold values from -40 to 40
- scores: bfloat16 [128, 524288], P('dom', 'param'), may hold values from -6 to 6
- basis: bfloat16 [524288, 128], P(('param', 'dom')), may hold values from -0.0078125 to 0.0078125
Outputs:
- velocity: bfloat16 [128, 524288], P('dom', 'param')
- phi: float32 [128, 128], P('dom')
All inputs are finite; a program needn't handle non-finite values.
Results may differ from a plain program's by a relative error of at most 0.0049.
Values may be sent and summed in bfloat16 or wider, within the bound.
A program may use at most 128 MiB of HBM per device.

v0:
```python
import math

import jax
import jax.numpy as jnp
from jax import lax
from jax.sharding import PartitionSpec as P

P_SIZE = 524288
R = 128


def stein_terms(own, every, every_score):
    count = every.shape[0]
    every_sq = jnp.sum(every * every, axis=1)
    own_sq = jnp.sum(own * own, axis=1)
    center = jnp.mean(every, axis=0)
    width = 2.0 * (jnp.mean(every_sq) - jnp.sum(center * center)) / math.log(count) + 1e-06
    cross = jnp.dot(own, every.T, precision=lax.Precision.HIGHEST)
    dist = own_sq[:, None] + every_sq[None, :] - 2.0 * cross
    kern = jnp.exp(-dist / width)
    drive = jnp.dot(kern, every_score, precision=lax.Precision.HIGHEST)
    pull = jnp.dot(kern, every, precision=lax.Precision.HIGHEST)
    total = jnp.sum(kern, axis=1)
    return (drive + 2.0 / width * (own * total[:, None] - pull)) / count


def lift_rows(phi_rows, basis_rows):
    lifted = lax.dot_general(
        phi_rows.astype(jnp.bfloat16),
        basis_rows,
        (((1,), (1,)), ((), ())),
        preferred_element_type=jnp.float32,
    )
    return (lifted * math.sqrt(P_SIZE / R)).astype(jnp.bfloat16)


def body(particles, scores, basis):
    rows = particles.shape[0]
    first = lax.axis_index("dom") * rows
    block_basis = lax.all_gather(basis, "dom", axis=0, tiled=True)
    partial_c = jnp.dot(particles, block_basis, preferred_element_type=jnp.float32)
    partial_s = jnp.dot(scores, block_basis, preferred_element_type=jnp.float32)
    summed_c, summed_s = lax.psum((partial_c, partial_s), "param")
    every, every_score = (
        lax.all_gather(summed_c, "dom", axis=0, tiled=True),
        lax.all_gather(summed_s, "dom", axis=0, tiled=True),
    )
    own = lax.dynamic_slice_in_dim(every, first, rows, 0)
    phi = stein_terms(own, every, every_score)
    velocity = lift_rows(phi, block_basis)
    return (velocity, phi)


def solution(mesh):
    in_specs = (P("dom", "param"), P("dom", "param"), P(("param", "dom"), None))
    out_specs = (P("dom", "param"), P("dom", None))
    return jax.shard_map(body, mesh=mesh, in_specs=in_specs, out_specs=out_specs, check_vma=False)
```

profile of v0, /device:TPU:0, one launch (start us, length us, event | category | flops | bytes accessed | tf_op | source)
XLA Modules:
  0.0 398.4 jit_solution(16221415659514092032)
XLA Ops:
  7.2 0.0 all-gather.2.cloned.1.call-start
  7.2 0.7 all-gather.2.cloned.1.call-update
  7.9 293.0 %all-gather.2.cloned.1.call-done = bf16[131072,128]{1,0:T(8,128)(2,1)} async-done(((bf16[16384,128]{1,0:T(8,128)(2,1)}), bf16[131072,128]{1,0:T(8,128)(2,1)}) %all-gather.2.cloned.1.call-update) | async-done | bytes 33554448 | tf_op jit(solution)/shard_map/all_gather | solution.py:40
  300.9 0.0 copy-start
  300.9 14.2 %fusion.13 = f32[16,128]{1,0:T(8,128)S(1)} fusion(bf16[16,131072]{1,0:T(8,128)(2,1)} %param.4, bf16[131072,128]{1,0:T(8,128)(2,1)} %all-gather.2.cloned.1.call-done), kind=kOutput, calls=%fused_computation.20 | convolution fusion | flops 536870912 | bytes 37756928 | tf_op jit(solution)/shard_map/dot_general | solution.py:42
  315.2 0.0 copy-done
  315.2 12.5 %fusion.12 = f32[16,128]{1,0:T(8,128)S(1)} fusion(bf16[16,131072]{1,0:T(8,128)(2,1)S(1)} %copy-done, bf16[131072,128]{1,0:T(8,128)(2,1)} %all-gather.2.cloned.1.call-done), kind=kOutput, calls=%fused_computation.19 | convolution fusion | flops 536870912 | bytes 37756928 | tf_op jit(solution)/shard_map/dot_general | solution.py:41
  327.6 16.0 %all-reduce = (f32[16,128]{1,0:T(8,128)S(1)}, f32[16,128]{1,0:T(8,128)S(1)}) all-reduce(f32[16,128]{1,0:T(8,128)S(1)} %fusion.12, f32[16,128]{1,0:T(8,128)S(1)} %fusion.13), channel_id=1, replica_groups=mesh['param'=4,'dom'=8] {'param'}, use_global_device_ids=true, to_apply=%region_0.0 | all-reduce | flops 4096 | bytes 32768 | tf_op jit(solution)/shard_map/psum | solution.py:43
  343.6 14.0 %all_gather.10 = f32[128,128]{1,0:T(8,128)S(1)} all-gather(f32[16,128]{1,0:T(8,128)S(1)} %get-tuple-element.5), channel_id=1, replica_groups=mesh['param'=4,'dom'=8] {'dom'}, dimensions={0}, use_global_device_ids=true | all-gather | bytes 73728 | tf_op jit(solution)/shard_map/all_gather | solution.py:45
  357.6 0.6 multiply_reduce_fusion.1
  358.2 0.1 multiply_reduce_fusion.2
  358.3 0.6 multiply_reduce_fusion.3
  358.9 14.0 %all_gather.11 = f32[128,128]{1,0:T(8,128)S(1)} all-gather(f32[16,128]{1,0:T(8,128)S(1)} %get-tuple-element.6), channel_id=1, replica_groups=mesh['param'=4,'dom'=8] {'dom'}, dimensions={0}, use_global_device_ids=true | all-gather | bytes 73728 | tf_op jit(solution)/shard_map/all_gather | solution.py:46
  374.3 0.3 fusion.11
  374.6 0.2 fusion.14
  374.8 0.2 fusion.3
  375.0 0.0 copy-start.1
  375.0 16.6 %fusion = bf16[16,131072]{1,0:T(8,128)(2,1)} fusion(bf16[131072,128]{1,0:T(8,128)(2,1)} %all-gather.2.cloned.1.call-done, f32[16,128]{1,0:T(8,128)S(1)} %fusion.3), kind=kOutput, calls=%fused_computation.1 | convolution fusion | flops 541067264 | bytes 37756928 | tf_op jit(solution)/shard_map/dot_general | solution.py:28
  391.6 0.0 copy-done.1
Async XLA Ops:
  7.2 293.8 %all-gather.2.cloned.1.call-start = ((), (), s32[]{:S(2)}) async-start(), calls=%async_computation | async-start | bytes 37748736 | tf_op jit(solution)/shard_map/all_gather | solution.py:40
  300.9 14.2 %copy-start = (bf16[16,131072]{1,0:T(8,128)(2,1)S(1)}, bf16[16,131072]{1,0:T(8,128)(2,1)}, u32[]{:S(2)}) copy-start(bf16[16,131072]{1,0:T(8,128)(2,1)} %param.3) | copy-start | bytes 12582916
  375.0 16.6 %copy-start.1 = (f32[16,128]{1,0:T(8,128)}, f32[16,128]{1,0:T(8,128)S(1)}, u32[]{:S(2)}) copy-start(f32[16,128]{1,0:T(8,128)S(1)} %fusion.3) | copy-start | bytes 24580
Sparse Core Ops, SparseCore 0:
  9.6 291.3 all-gather.1
where the time goes:
time: 399 us; the launch traced here: 398 us
  waiting for transfers between devices  294 us (74%)
  matrix products  44 us (11%)
  blocking collectives  43.9 us (11%)
  between operations  15.4 us (4%)
    all_gather x1, waiting for transfers between devices, body(): block_basis = lax.all_gather(basis, 'dom', axis=0, tiled=True)  293 us
    dot_general x1, matrix products, lift_rows(): lax.dot_general(phi_rows.astype(jnp.bfloat16), basis_rows, (((1,), (1,)),...  16.6 us
    psum x1, blocking collectives, body(): summed_c, summed_s = lax.psum((partial_c, partial_s), 'param')  16 us
    dot_general x1, matrix products, body(): partial_s = jnp.dot(scores, block_basis, preferred_element_type=jnp.float32)  14.2 us
    all_gather x1, blocking collectives, body(): lax.all_gather(summed_c, 'dom', axis=0, tiled=True)  14 us
    all_gather x1, blocking collectives, body(): lax.all_gather(summed_s, 'dom', axis=0, tiled=True)  14 us
    dot_general x1, matrix products, body(): jnp.dot(particles, block_basis, preferred_element_type=jnp.float32)  12.5 us
  transfers between devices with their start and end apart: 1, of which 1 were waited for; matrix products, arithmetic and copies ran while one was open for 0% of the time, Pallas kernels for 0%

commit v1 on v0

v1 whole, which is shorter than its diff:
```python
import functools
import math

import jax
import jax.numpy as jnp
from jax import lax
from jax.experimental import pallas as pl
from jax.experimental.pallas import tpu as pltpu
from jax.sharding import PartitionSpec as P

MESH = pl.DeviceIdType.MESH
HIGH = lax.Precision.HIGHEST
NT = (((1,), (1,)), ((), ()))


def stein_rows(own, every, every_score):
    count = every.shape[0]
    square = every * every
    every_sq = lax.dot_general(
        jnp.ones((8, every.shape[1]), jnp.float32), square, NT, precision=HIGH
    )[0:1, :]
    own_sq = jnp.sum(own * own, axis=1, keepdims=True)
    center = jnp.mean(every, axis=0, keepdims=True)
    spread = jnp.sum(square) / count - jnp.sum(center * center)
    width = 2.0 * spread / math.log(count) + 1e-06
    cross = lax.dot_general(own, every, NT, precision=HIGH)
    dist = own_sq + every_sq - 2.0 * cross
    kern = jnp.exp(-dist / width)
    drive = jnp.dot(kern, every_score, precision=HIGH)
    pull = jnp.dot(kern, every, precision=HIGH)
    total = jnp.sum(kern, axis=1, keepdims=True)
    return (drive + 2.0 / width * (own * total - pull)) / count


def kernel(
    n_p, n_d, rows, depth, cr, lift,
    part_ref, score_ref, basis_ref, vel_ref, phi_ref,
    held, ps, hps, vst, hv, acc, hacc, hpart, parts, every,
    in_sem, right_send, left_send, right_recv, left_recv,
    mate_send, mate_recv, aid_send, aid_recv, hp_send, hp_recv,
    pa_send, pa_recv, ev_send, ev_recv, v_sem, hv_send, hv_recv,
):
    p = lax.axis_index("param")
    d = lax.axis_index("dom")
    z, c = d // 2, lax.rem(d, 2)
    nz = n_d // 2
    aid = nz >= 4
    steps = nz - 2 if aid else nz - 1
    kk = depth // cr
    mate = 2 * z + 1 - c
    low_help, high_help = z == 1, z == nz - 2
    helper = jnp.logical_or(low_help, high_help)
    helped = jnp.logical_or(z == 0, z == nz - 1)
    client = jnp.where(low_help, c, n_d - 2 + c)
    server = jnp.where(z == 0, 2 + c, n_d - 4 + c)
    far = jnp.where(jnp.logical_or(low_help, z == 0), nz - 1, 0)
    wide = 2 * depth

    barrier = pltpu.get_barrier_semaphore()
    for i in range(1, n_p):
        pl.semaphore_signal(barrier, inc=1, device_id=(lax.rem(p + i, n_p), d), device_id_type=MESH)
    for i in range(1, n_d):
        pl.semaphore_signal(barrier, inc=1, device_id=(p, lax.rem(d + i, n_d)), device_id_type=MESH)

    def chunk(block, k):
        return pl.ds(pl.multiple_of(block * depth + k * cr, cr), cr)

    def remote(src, dst, ss, rs, dom):
        return pltpu.make_async_remote_copy(
            src_ref=src, dst_ref=dst, send_sem=ss, recv_sem=rs,
            device_id=(p, dom), device_id_type=MESH,
        )

    own_in = pltpu.make_async_copy(
        basis_ref, held.at[pl.ds(pl.multiple_of(d * depth, depth), depth)], in_sem.at[0])
    part_in = pltpu.make_async_copy(part_ref, ps.at[pl.ds(0, rows)], in_sem.at[1])
    score_in = pltpu.make_async_copy(score_ref, ps.at[pl.ds(rows, rows)], in_sem.at[2])
    own_in.start()
    part_in.start()
    score_in.start()
    pl.semaphore_wait(barrier, n_p + n_d - 2)

    right_ok, left_ok = z < nz - 1, z > 0

    def right_copy(s, k):
        src = basis_ref.at[pl.ds(pl.multiple_of(k * cr, cr), cr)] if s == 0 else held.at[chunk(d - 2 * s, k)]
        return remote(src, held.at[chunk(d - 2 * s, k)], right_send.at[s, k], right_recv.at[s, k], d + 2)

    def left_copy(s, k):
        src = basis_ref.at[pl.ds(pl.multiple_of(k * cr, cr), cr)] if s == 0 else held.at[chunk(d + 2 * s, k)]
        return remote(src, held.at[chunk(d + 2 * s, k)], left_send.at[s, k], left_recv.at[s, k], d - 2)

    def from_left(s, k):
        at = held.at[chunk(d - 2 * s - 2, k)]
        return remote(at, at, right_send.at[s, k], right_recv.at[s, k], d - 2)

    def from_right(s, k):
        at = held.at[chunk(d + 2 * s + 2, k)]
        return remote(at, at, left_send.at[s, k], left_recv.at[s, k], d + 2)

    def mate_copy(slot, block, k):
        src = basis_ref.at[pl.ds(pl.multiple_of(k * cr, cr), cr)] if slot == 0 else held.at[chunk(block, k)]
        return remote(src, held.at[chunk(block, k)], mate_send.at[slot, k], mate_recv.at[slot, k], mate)

    def from_mate(slot, block, k):
        at = held.at[chunk(block, k)]
        return remote(at, at, mate_send.at[slot, k], mate_recv.at[slot, k], mate)

    def aid_copy(i):
        src = (part_ref, score_ref)[i].at[:, pl.ds(pl.multiple_of(far * wide, wide), wide)]
        return remote(src, hps.at[pl.ds(i * rows, rows)], aid_send.at[i], aid_recv.at[i], server)

    def aid_arrival(i):
        at = hps.at[pl.ds(i * rows, rows)]
        return remote(at, at, aid_send.at[i], aid_recv.at[i], client)

    def each_chunk(body):
        @pl.loop(0, kk)
        def _(k):
            body(k)

    def start_own(k):
        @pl.when(right_ok)
        def _():
            right_copy(0, k).start()

        @pl.when(left_ok)
        def _():
            left_copy(0, k).start()

        mate_copy(0, d, k).start()

    each_chunk(start_own)
    if aid:
        @pl.when(helped)
        def _():
            for i in range(2):
                aid_copy(i).start()

    acc[...] = jnp.zeros_like(acc)
    hacc[...] = jnp.zeros_like(hacc)
    own_in.wait()
    part_in.wait()
    score_in.wait()

    def use(block, k, last=False):
        got = held[chunk(block, k), :]
        acc[...] += jnp.dot(ps[:, chunk(block, k)], got, preferred_element_type=jnp.float32)
        if aid and last:
            @pl.when(jnp.logical_and(helper, block // 2 == far))
            def _():
                hacc[...] += jnp.dot(
                    hps[:, chunk(lax.rem(block, 2), k)], held[chunk(block, k), :],
                    preferred_element_type=jnp.float32)

    def use_own(k):
        use(d, k)
        from_mate(0, mate, k).wait_recv()
        use(mate, k)

    each_chunk(use_own)

    for s in range(steps):
        last = s == steps - 1
        has_left, has_right = z >= s + 1, z + s + 1 < nz
        if aid and last:
            @pl.when(helper)
            def _():
                for i in range(2):
                    aid_arrival(i).wait_recv()

        def arrive(k, s=s, last=last, has_left=has_left, has_right=has_right):
            @pl.when(has_left)
            def _():
                from_left(s, k).wait_recv()
                if not last:
                    @pl.when(right_ok)
                    def _():
                        right_copy(s + 1, k).start()
                mate_copy(1 + 2 * s, d - 2 * s - 2, k).start()

            @pl.when(has_right)
            def _():
                from_right(s, k).wait_recv()
                if not last:
                    @pl.when(left_ok)
                    def _():
                        left_copy(s + 1, k).start()
                mate_copy(2 + 2 * s, d + 2 * s + 2, k).start()

            @pl.when(has_left)
            def _():
                use(d - 2 * s - 2, k, last)
                from_mate(1 + 2 * s, mate - 2 * s - 2, k).wait_recv()
                use(mate - 2 * s - 2, k, last)

            @pl.when(has_right)
            def _():
                use(d + 2 * s + 2, k, last)
                from_mate(2 + 2 * s, mate + 2 * s + 2, k).wait_recv()
                use(mate + 2 * s + 2, k, last)

        each_chunk(arrive)

    if aid:
        give = remote(hacc, hpart, hp_send, hp_recv, client)
        take = remote(hacc, hpart, hp_send, hp_recv, server)

        @pl.when(helper)
        def _():
            give.start()

        @pl.when(helped)
        def _():
            take.wait_recv()
            acc[...] += hpart[...]

    parts[pl.ds(p, 1)] = acc[...][None]
    pa = []
    for i in range(1, n_p):
        copy = pltpu.make_async_remote_copy(
            src_ref=acc, dst_ref=parts.at[p], send_sem=pa_send.at[i], recv_sem=pa_recv.at[i],
            device_id=(lax.rem(p + i, n_p), d), device_id_type=MESH)
        copy.start()
        pa.append(copy)
    for i in range(1, n_p):
        src = lax.rem(p + n_p - i, n_p)
        pltpu.make_async_remote_copy(
            src_ref=acc, dst_ref=parts.at[src], send_sem=pa_send.at[i], recv_sem=pa_recv.at[i],
            device_id=(src, d), device_id_type=MESH).wait_recv()
    whole = parts[0]
    for i in range(1, n_p):
        whole = whole + parts[i]
    every[pl.ds(d, 1)] = whole[None]
    ev = []
    for i in range(1, n_d):
        copy = remote(every.at[d], every.at[d], ev_send.at[i], ev_recv.at[i], lax.rem(d + i, n_d))
        copy.start()
        ev.append(copy)
    for i in range(1, n_d):
        src = lax.rem(d + n_d - i, n_d)
        remote(every.at[src], every.at[src], ev_send.at[i], ev_recv.at[i], src).wait_recv()

    count, rank = n_d * rows, acc.shape[1]
    coeffs = every[:, 0:rows, :].reshape(count, rank)
    score_coeffs = every[:, rows:2 * rows, :].reshape(count, rank)
    mine = every[d, 0:rows, :]
    if aid:
        theirs = every[jnp.where(helper, client, d), 0:rows, :]
        phi = stein_rows(jnp.concatenate([mine, theirs], axis=0), coeffs, score_coeffs)
    else:
        phi = stein_rows(mine, coeffs, score_coeffs)
    phi_ref[...] = phi[0:rows]
    low = phi.astype(jnp.bfloat16)

    def lifted(rows_of, block, k):
        up = lax.dot_general(rows_of, held[chunk(block, k), :], NT, preferred_element_type=jnp.float32)
        return (up * lift).astype(jnp.bfloat16)

    if aid:
        def back(j, i):
            at = chunk(j, i)
            there = vel_ref.at[:, chunk(2 * far + j, i)]
            return remote(hv.at[:, at], there, hv_send.at[j, i], hv_recv.at[j, i], client)

        def back_arrival(j, i):
            there = vel_ref.at[:, chunk(2 * far + j, i)]
            return remote(hv.at[:, chunk(j, i)], there, hv_send.at[j, i], hv_recv.at[j, i], server)

        @pl.when(helper)
        def _():
            for j in range(2):
                def send_back(k, j=j):
                    hv[:, chunk(j, k)] = lifted(low[rows:2 * rows], 2 * far + j, k)
                    back(j, k).start()

                each_chunk(send_back)

    def out_copy(block, k):
        return pltpu.make_async_copy(vst.at[:, chunk(block, k)], vel_ref.at[:, chunk(block, k)], v_sem.at[block, k])

    def both(body):
        @pl.loop(0, n_d)
        def _(block):
            def one():
                each_chunk(lambda k: body(block, k))

            if aid:
                pl.when(jnp.logical_not(jnp.logical_and(helped, block // 2 == far)))(one)
            else:
                one()

    def write(block, k):
        vst[:, chunk(block, k)] = lifted(low[0:rows], block, k)
        out_copy(block, k).start()

    both(write)

    def end_own(k):
        @pl.when(right_ok)
        def _():
            right_copy(0, k).wait_send()

        @pl.when(left_ok)
        def _():
            left_copy(0, k).wait_send()

        mate_copy(0, d, k).wait_send()

    each_chunk(end_own)
    for s in range(steps):
        last = s == steps - 1
        has_left, has_right = z >= s + 1, z + s + 1 < nz

        def end(k, s=s, last=last, has_left=has_left, has_right=has_right):
            @pl.when(has_left)
            def _():
                if not last:
                    @pl.when(right_ok)
                    def _():
                        right_copy(s + 1, k).wait_send()
                mate_copy(1 + 2 * s, d - 2 * s - 2, k).wait_send()

            @pl.when(has_right)
            def _():
                if not last:
                    @pl.when(left_ok)
                    def _():
                        left_copy(s + 1, k).wait_send()
                mate_copy(2 + 2 * s, d + 2 * s + 2, k).wait_send()

        each_chunk(end)
    for copy in pa + ev:
        copy.wait_send()
    both(lambda block, k: out_copy(block, k).wait())
    if aid:
        @pl.when(helper)
        def _():
            give.wait_send()
            for j in range(2):
                each_chunk(lambda k, j=j: back(j, k).wait_send())

        @pl.when(helped)
        def _():
            for i in range(2):
                aid_copy(i).wait_send()
            for j in range(2):
                each_chunk(lambda k, j=j: back_arrival(j, k).wait_recv())


def solution(mesh):
    n_p, n_d = mesh.shape["param"], mesh.shape["dom"]

    def body(particles, scores, basis):
        rows, dims = particles.shape
        depth, rank = basis.shape
        cr = min(depth, 2048)
        kk = depth // cr
        nz = n_d // 2
        f32, bf16 = jnp.float32, jnp.bfloat16
        dma = pltpu.SemaphoreType.DMA
        anywhere = pl.BlockSpec(memory_space=pl.ANY)
        lift = math.sqrt(dims * n_p / rank)
        return pl.pallas_call(
            functools.partial(kernel, n_p, n_d, rows, depth, cr, lift),
            out_shape=(
                jax.ShapeDtypeStruct((rows, dims), bf16),
                jax.ShapeDtypeStruct((rows, rank), f32),
            ),
            in_specs=[anywhere] * 3,
            out_specs=(anywhere, pl.BlockSpec(memory_space=pltpu.VMEM)),
            scratch_shapes=[
                pltpu.VMEM((dims, rank), bf16),
                pltpu.VMEM((2 * rows, dims), bf16),
                pltpu.VMEM((2 * rows, 2 * depth), bf16),
                pltpu.VMEM((rows, dims), bf16),
                pltpu.VMEM((rows, 2 * depth), bf16),
                pltpu.VMEM((2 * rows, rank), f32),
                pltpu.VMEM((2 * rows, rank), f32),
                pltpu.VMEM((2 * rows, rank), f32),
                pltpu.VMEM((n_p, 2 * rows, rank), f32),
                pltpu.VMEM((n_d, 2 * rows, rank), f32),
                dma((3,)),
                dma((nz, kk)), dma((nz, kk)), dma((nz, kk)), dma((nz, kk)),
                dma((2 * nz, kk)), dma((2 * nz, kk)),
                dma((2,)), dma((2,)), dma, dma,
                dma((n_p,)), dma((n_p,)), dma((n_d,)), dma((n_d,)),
                dma((n_d, kk)), dma((2, kk)), dma((2, kk)),
            ],
            compiler_params=pltpu.CompilerParams(
                collective_id=0, has_side_effects=True, vmem_limit_bytes=60 * 1024 * 1024
            ),
        )(particles, scores, basis)

    in_specs = (P("dom", "param"), P("dom", "param"), P(("param", "dom"), None))
    out_specs = (P("dom", "param"), P("dom", None))
    return jax.shard_map(body, mesh=mesh, in_specs=in_specs, out_specs=out_specs, check_vma=False)
```

time: 399 us -> 234 us (0.59)
  waiting for transfers between devices: 294 us -> 0 us
  Pallas kernels: 0 us -> 228 us
  matrix products: 44 us -> 0 us
  blocking collectives: 43.9 us -> 0 us
  between operations: 15.4 us -> 0.65 us
  local copies, waits for them, and re-layouts: 0.01 us -> 5.08 us
    all_gather x1 -> x0, waiting for transfers between devices: 293 us -> none  [body(): block_basis = lax.all_gather(basis, 'dom', axis=0, tiled=True)]
    pallas_call x0 -> x1, Pallas kernels: none -> 228 us  [body(): pl.pallas_call(functools.partial(kernel, n_p, n_d, rows, depth, cr, lift)...]
    dot_general x6 -> x0, matrix products: 44 us -> none  [the longest x1 16.6 us: lift_rows(): lax.dot_general(phi_rows.astype(jnp.bfloat16), basis_rows, (((1,), (1,)),...]
    all_gather x2 -> x0, blocking collectives: 27.9 us -> none  [the longest x1 14 us: body(): lax.all_gather(summed_c, 'dom', axis=0, tiled=True)]
    psum x1 -> x0, blocking collectives: 16 us -> none  [body(): summed_c, summed_s = lax.psum((partial_c, partial_s), 'param')]
    unnamed x4, local copies, waits for them, and re-layouts: 0.01 us -> 5.08 us
  transfers between devices with their start and end apart: 1 -> 0, of which waited for: 1 -> 0; matrix products, arithmetic and copies ran while one was open for 0% -> 0% of each run, Pallas kernels for 0% -> 0%
where the time goes in v1:
time: 234 us
  Pallas kernels  228 us (97%)
  local copies, waits for them, and re-layouts  5.08 us (2%)
    pallas_call x1, Pallas kernels, body(): pl.pallas_call(functools.partial(kernel, n_p, n_d, rows, depth, cr, lift)...  228 us
    unnamed x4, local copies, waits for them, and re-layouts  5.08 us

profile of v1, /device:TPU:0, one launch (start us, length us, event | category | flops | bytes accessed | tf_op | source)
XLA Modules:
  0.0 233.6 jit_solution(16660908775278152240)
XLA Ops:
  0.6 227.9 %shard_map.50 = (bf16[16,131072]{1,0:T(8,128)(2,1)}, f32[16,128]{1,0:T(8,128)}) custom-call(bf16[16,131072]{1,0:T(8,128)(2,1)} %part_ref.1, bf16[16,131072]{1,0:T(8,128)(2,1)} %score_ref.1, bf16[16384,128]{1,0:T(8,128)(2,1)} %basis_ref.1), custom_call_target="tpu_custom_call" | custom-call | tf_op jit(solution)/shard_map/pallas_call | solution.py:364
  228.5 0.0 copy-start
  228.5 4.5 %copy.7 = bf16[16,131072]{1,0:T(8,128)(2,1)} copy(bf16[16,131072]{1,0:T(8,128)(2,1)} %get-tuple-element.4) | data formatting | bytes 8388608
  233.0 0.0 copy-done
  233.0 0.6 copy.8
Async XLA Ops:
  228.5 4.5 %copy-start = (f32[16,128]{1,0:T(8,128)S(1)}, f32[16,128]{1,0:T(8,128)}, u32[]{:S(2)}) copy-start(f32[16,128]{1,0:T(8,128)} %get-tuple-element.5) | copy-start | bytes 24580

commit v2 on v1

--- a/solution.py
+++ b/solution.py
@@ -131,12 +131,6 @@
         mate_copy(0, d, k).start()
 
     each_chunk(start_own)
-    if aid:
-        @pl.when(helped)
-        def _():
-            for i in range(2):
-                aid_copy(i).start()
-
     acc[...] = jnp.zeros_like(acc)
     hacc[...] = jnp.zeros_like(hacc)
     own_in.wait()
@@ -201,6 +195,11 @@
                 use(mate + 2 * s + 2, k, last)
 
         each_chunk(arrive)
+        if aid and s == 0:
+            @pl.when(helped)
+            def _():
+                for i in range(2):
+                    aid_copy(i).start()
 
     if aid:
         give = remote(hacc, hpart, hp_send, hp_recv, client)
@@ -253,9 +252,34 @@
     phi_ref[...] = phi[0:rows]
     low = phi.astype(jnp.bfloat16)
 
-    def lifted(rows_of, block, k):
-        up = lax.dot_general(rows_of, held[chunk(block, k), :], NT, preferred_element_type=jnp.float32)
+    half = cr // 2
+
+    def spread(rows_of):
+        blank = jnp.zeros_like(rows_of)
+        upper = jnp.concatenate([rows_of, blank], axis=1)
+        lower = jnp.concatenate([blank, rows_of], axis=1)
+        return jnp.concatenate([upper, lower], axis=0)
+
+    def lifted(spread_rows, block, k):
+        start = pl.multiple_of(block * depth + k * cr, cr)
+        first, second = held[pl.ds(start, half), :], held[pl.ds(pl.multiple_of(start + half, half), half), :]
+        up = lax.dot_general(
+            spread_rows, jnp.concatenate([first, second], axis=1), NT,
+            preferred_element_type=jnp.float32)
         return (up * lift).astype(jnp.bfloat16)
+
+    def halves(j, k):
+        start = pl.multiple_of(j * depth + k * cr, cr)
+        return pl.ds(start, half), pl.ds(pl.multiple_of(start + half, half), half)
+
+    def out_copy(block, k):
+        return pltpu.make_async_copy(vst.at[:, chunk(block, k)], vel_ref.at[:, chunk(block, k)], v_sem.at[block, k])
+
+    def keep(up, block, k, total):
+        left, right = halves(block, k)
+        vst[:, left] = up[0:rows]
+        vst[:, right] = up[total:total + rows]
+        out_copy(block, k).start()
 
     if aid:
         def back(j, i):
@@ -269,32 +293,35 @@
 
         @pl.when(helper)
         def _():
+            low_both = spread(low)
             for j in range(2):
                 def send_back(k, j=j):
-                    hv[:, chunk(j, k)] = lifted(low[rows:2 * rows], 2 * far + j, k)
+                    up = lifted(low_both, 2 * far + j, k)
+                    left, right = halves(j, k)
+                    hv[:, left] = up[rows:2 * rows]
+                    hv[:, right] = up[3 * rows:4 * rows]
                     back(j, k).start()
+                    keep(up, 2 * far + j, k, 2 * rows)
 
                 each_chunk(send_back)
 
-    def out_copy(block, k):
-        return pltpu.make_async_copy(vst.at[:, chunk(block, k)], vel_ref.at[:, chunk(block, k)], v_sem.at[block, k])
-
-    def both(body):
+    def both(body, skip):
         @pl.loop(0, n_d)
         def _(block):
             def one():
                 each_chunk(lambda k: body(block, k))
 
             if aid:
-                pl.when(jnp.logical_not(jnp.logical_and(helped, block // 2 == far)))(one)
+                pl.when(jnp.logical_not(jnp.logical_and(skip, block // 2 == far)))(one)
             else:
                 one()
 
+    low_own = spread(low[0:rows])
+
     def write(block, k):
-        vst[:, chunk(block, k)] = lifted(low[0:rows], block, k)
-        out_copy(block, k).start()
-
-    both(write)
+        keep(lifted(low_own, block, k), block, k, rows)
+
+    both(write, jnp.logical_or(helper, helped))
 
     def end_own(k):
         @pl.when(right_ok)
@@ -332,7 +359,7 @@
         each_chunk(end)
     for copy in pa + ev:
         copy.wait_send()
-    both(lambda block, k: out_copy(block, k).wait())
+    both(lambda block, k: out_copy(block, k).wait(), helped)
     if aid:
         @pl.when(helper)
         def _():
@@ -388,7 +415,7 @@
                 dma((n_d, kk)), dma((2, kk)), dma((2, kk)),
             ],
             compiler_params=pltpu.CompilerParams(
-                collective_id=0, has_side_effects=True, vmem_limit_bytes=60 * 1024 * 1024
+                collective_id=0, has_side_effects=True, vmem_limit_bytes=50 * 1024 * 1024
             ),
         )(particles, scores, basis)
 

time: 234 us -> 233 us (level)
    unnamed x4 -> x2, local copies, waits for them, and re-layouts: 5.08 us -> 5.07 us
where the time goes in v2:
time: 233 us
  Pallas kernels  227 us (97%)
  local copies, waits for them, and re-layouts  5.07 us (2%)
    pallas_call x1, Pallas kernels, body(): pl.pallas_call(functools.partial(kernel, n_p, n_d, rows, depth, cr, lift)...  227 us
    unnamed x2, local copies, waits for them, and re-layouts  5.07 us

profile of v2, /device:TPU:0, one launch (start us, length us, event | category | flops | bytes accessed | tf_op | source)
XLA Modules:
  0.0 233.0 jit_solution(12518264352122844049)
XLA Ops:
  0.6 227.3 %shard_map.50 = (bf16[16,131072]{1,0:T(8,128)(2,1)}, f32[16,128]{1,0:T(8,128)S(1)}) custom-call(bf16[16,131072]{1,0:T(8,128)(2,1)} %part_ref.1, bf16[16,131072]{1,0:T(8,128)(2,1)} %score_ref.1, bf16[16384,128]{1,0:T(8,128)(2,1)} %basis_ref.1), custom_call_target="tpu_custom_call" | custom-call | tf_op jit(solution)/shard_map/pallas_call | solution.py:391
  227.9 4.5 %copy.7 = bf16[16,131072]{1,0:T(8,128)(2,1)} copy(bf16[16,131072]{1,0:T(8,128)(2,1)} %get-tuple-element.4) | data formatting | bytes 8388608
  232.4 0.6 copy.8
